TPU v7x, 32 devices: a whole 2x2x4 slice. The times are simulated.
32 devices in a mesh: pb: 4 (over y, core), pa: 8 (over z, x).
Axes of the slice: x: 2, y: 2, z: 4, core: 2. Of those that a mesh axis runs over, the one named last changes fastest.
Arguments:
- query_hidden: bfloat16 [32, 32, 2048], P('pb', 'pa'), may hold values from -32 to 32
- page_hidden: bfloat16 [8, 1024, 2048], P('pa', 'pb'), may hold values from -4.2 to 4.2
- projection: bfloat16 [2048, 128], replicated, may hold values from -0.125 to 0.125
- clicks: int32 [32, 8, 2], P('pb'), may hold values from 0 to 7, as said below
- bins: int32 [32, 8], P('pb'), may hold values from 0 to 7
Outputs:
- query_grad: bfloat16 [32, 32, 2048], P('pb', 'pa')
- page_grad: bfloat16 [8, 1024, 2048], P('pa', 'pb')
- weight_grad: float32 [2048, 128], P(('pb', 'pa'))
Inputs may be any that keep to these rules, and one draw needn't show every extreme that they name: `clicks`: the two pages of a pair always differ.
All inputs are finite; a program needn't handle non-finite values.
Results may differ from a plain program's by a relative error of at most 0.019.
Values may be sent and summed in bfloat16 or wider, within the bound.
A program may use at most 64 MiB of HBM per device.

v0:
```python
import jax
import jax.numpy as jnp
from jax import lax
from jax.sharding import PartitionSpec as P

sharpness = 0.25


def from_behind(value, axis, steps):
    count = lax.axis_size(axis)
    pairs = [(source, (source + steps) % count) for source in range(count)]
    return lax.ppermute(value, axis, pairs)


def logits(token_rows, patch_rows):
    return sharpness * lax.dot_general(
        token_rows, patch_rows, (((1,), (1,)), ((), ())), preferred_element_type=jnp.float32
    )


def shards(query_hidden, page_hidden, projection, clicks, bins):
    query_count, token_local, hidden_width = query_hidden.shape
    page_count, patch_local, _ = page_hidden.shape
    embed_width = projection.shape[1]
    own_embed = jnp.dot(
        query_hidden.reshape(-1, hidden_width), projection, preferred_element_type=jnp.float32
    ).astype(jnp.bfloat16)
    own_embed = own_embed.reshape(query_count, token_local, embed_width)
    tok_rows = lax.all_gather(own_embed, "pa", axis=1, tiled=True).reshape(-1, embed_width)
    row_count = tok_rows.shape[0]
    query_tokens = row_count // query_count
    page_embed = jnp.dot(
        page_hidden.reshape(-1, hidden_width), projection, preferred_element_type=jnp.float32
    ).astype(jnp.bfloat16)
    page_embed = page_embed.reshape(page_count, patch_local, embed_width)
    start_state = (
        jnp.full((row_count, page_count), -1e30, jnp.float32),
        jnp.zeros((row_count, page_count), jnp.float32),
    )
    run_max, run_sum = start_state
    logit_block = logits(tok_rows, lax.all_gather(page_embed, "pb", axis=1, tiled=True)[0])
    new_max = jnp.maximum(run_max[:, 0], jnp.max(logit_block, axis=1))
    new_sum = run_sum[:, 0] * jnp.exp(run_max[:, 0] - new_max)
    new_sum = new_sum + jnp.sum(jnp.exp(logit_block - new_max[:, None]), axis=1)
    max_list = [new_max]
    sum_list = [new_sum]
    run_max = jnp.stack(max_list, axis=1)
    run_sum = jnp.stack(sum_list, axis=1)
    log_norm = run_max + jnp.log(run_sum)
    query_score = log_norm.reshape(query_count, query_tokens, page_count).sum(axis=1)
    owned_pages = lax.axis_index("pa") * page_count + jnp.arange(page_count, dtype=jnp.int32)
    positive = clicks[:, :, 0]
    negative = clicks[:, :, 1]
    hit_pos = (positive[:, :, None] == owned_pages).astype(jnp.float32)
    hit_neg = (negative[:, :, None] == owned_pages).astype(jnp.float32)
    score_table = lax.all_gather(query_score, "pa", axis=1, tiled=True)
    page_ids = jnp.arange(score_table.shape[1], dtype=jnp.int32)
    table_pos = (positive[:, :, None] == page_ids).astype(jnp.float32)
    table_neg = (negative[:, :, None] == page_ids).astype(jnp.float32)
    pair_gap = jnp.sum(table_pos * score_table[:, None, :], axis=2) - jnp.sum(
        table_neg * score_table[:, None, :], axis=2
    )
    pair_weight = jnp.sqrt(bins.astype(jnp.float32) + 1.0)
    pair_coeff = -pair_weight * jax.nn.sigmoid(-pair_gap)
    score_grad = jnp.sum(pair_coeff[:, :, None] * (hit_pos - hit_neg), axis=1)
    grad_rows = jnp.repeat(score_grad, query_tokens, axis=0)
    norm_cols = jnp.repeat(log_norm, patch_local, axis=1)
    grad_cols = jnp.repeat(grad_rows, patch_local, axis=1)

    def cycle_turn(turn_index, cycle_state):
        patch_block, patch_accum, token_acc = cycle_state
        block_rows = patch_block.reshape(-1, embed_width)
        logit_block = logits(tok_rows, block_rows)
        soft_grad = (grad_cols * jnp.exp(logit_block - norm_cols)).astype(jnp.bfloat16)
        token_acc = token_acc + jnp.dot(soft_grad, block_rows, preferred_element_type=jnp.float32)
        patch_part = lax.dot_general(
            soft_grad, tok_rows, (((0,), (0,)), ((), ())), preferred_element_type=jnp.float32
        )
        patch_accum = patch_accum + patch_part.reshape(patch_accum.shape)
        patch_block = from_behind(patch_block, "pb", 1)
        patch_accum = from_behind(patch_accum.astype(jnp.bfloat16), "pb", 1).astype(
            patch_accum.dtype
        )
        return (patch_block, patch_accum, token_acc)

    start_state = (
        page_embed,
        jnp.zeros(page_embed.shape, jnp.float32),
        jnp.zeros((row_count, embed_width), jnp.float32),
    )
    _, patch_acc, token_acc = lax.fori_loop(0, lax.axis_size("pb"), cycle_turn, start_state)
    token_own = lax.psum_scatter(
        token_acc.reshape(query_count, query_tokens, embed_width).astype(jnp.bfloat16),
        "pa",
        scatter_dimension=1,
        tiled=True,
    ).astype(jnp.float32)
    token_low = (sharpness * token_own).astype(jnp.bfloat16).reshape(-1, embed_width)
    patch_low = (sharpness * patch_acc).astype(jnp.bfloat16).reshape(-1, embed_width)
    query_grad = lax.dot_general(
        token_low, projection, (((1,), (1,)), ((), ())), preferred_element_type=jnp.float32
    )
    query_grad = query_grad.astype(jnp.bfloat16).reshape(query_hidden.shape)
    page_grad = lax.dot_general(
        patch_low, projection, (((1,), (1,)), ((), ())), preferred_element_type=jnp.float32
    )
    page_grad = page_grad.astype(jnp.bfloat16).reshape(page_hidden.shape)
    weight_term = lax.dot_general(
        query_hidden.reshape(-1, hidden_width),
        token_low,
        (((0,), (0,)), ((), ())),
        preferred_element_type=jnp.float32,
    )
    weight_term = weight_term + lax.dot_general(
        page_hidden.reshape(-1, hidden_width),
        patch_low,
        (((0,), (0,)), ((), ())),
        preferred_element_type=jnp.float32,
    )
    weight_grad = lax.psum_scatter(weight_term, ("pb", "pa"), scatter_dimension=0, tiled=True)
    return (query_grad, page_grad, weight_grad)


def solution(mesh):
    return jax.shard_map(
        shards,
        mesh=mesh,
        in_specs=(
            P("pb", "pa", None),
            P("pa", "pb", None),
            P(),
            P("pb", None, None),
            P("pb", None),
        ),
        out_specs=(P("pb", "pa", None), P("pa", "pb", None), P(("pb", "pa"), None)),
        check_vma=False,
    )
```

profile of v0, /device:TPU:0, one launch (start us, length us, event | category | flops | bytes accessed | tf_op | source)
XLA Modules:
  0.0 294.6 jit_solution(1814558097921956855)
XLA Ops:
  7.2 0.0 copy-start
  7.2 0.0 copy-start.2
  7.2 0.0 reduce-scatter.5.cloned.1.call-start
  7.2 1.2 copy-done
  8.4 1.5 convolution_convert_fusion.2
  9.9 7.3 %all-gather = bf16[1024,128]{1,0:T(8,128)(2,1)S(1)} all-gather(bf16[256,128]{1,0:T(8,128)(2,1)S(1)} %convolution_convert_fusion.2), channel_id=2, replica_groups=mesh['pb'=4,'pa'=8] {'pb'}, dimensions={0}, use_global_device_ids=true | all-gather | bytes 327680 | tf_op jit(solution)/shard_map/all_gather | solution.py:41
  17.2 0.0 copy-done.2
  17.2 0.2 convolution_convert_fusion.3
  17.5 30.9 %all_gather.9 = bf16[8,32,128]{2,0,1:T(8,128)(2,1)S(1)} all-gather(bf16[8,4,128]{2,0,1:T(8,128)(2,1)S(1)} %copy.36), channel_id=1, replica_groups=mesh['pb'=4,'pa'=8] {'pa'}, dimensions={1}, use_global_device_ids=true | all-gather | bytes 73728 | tf_op jit(solution)/shard_map/all_gather | solution.py:29
  48.3 0.0 copy-start.4
  48.4 0.0 copy-start.5
  48.4 0.4 fusion.24
  48.8 0.1 max_squeeze.20
  48.8 0.3 exponential_reduce_fusion
  49.1 0.1 reduce_sum.50
  49.3 0.1 add_reduce_fusion
  49.4 20.5 %all-gather.1 = f32[8,1,8]{2,1,0:T(1,128)S(1)} all-gather(f32[1,1,8]{2,1,0:T(1,128)S(1)} %bitcast.83), channel_id=1, replica_groups=mesh['pb'=4,'pa'=8] {'pa'}, dimensions={0}, use_global_device_ids=true | all-gather | bytes 288 | tf_op jit(solution)/shard_map/all_gather | solution.py:56
  69.8 0.1 copy.39
  69.9 0.0 copy-done.4
  69.9 0.2 select_reduce_fusion
  70.1 0.1 fusion.20
  70.2 0.1 broadcast_in_dim.24
  70.3 0.1 broadcast_in_dim.25
  70.4 18.0 %while.15 = (s32[]{:T(128)}, bf16[1,256,128]{2,1,0:T(8,128)(2,1)S(1)}, f32[1,256,128]{2,1,0:T(8,128)S(1)}, f32[256,128]{1,0:T(8,128)S(1)}, bf16[256,128]{1,0:T(8...) while((s32[]{:T(128)}, bf16[1,256,128]{2,1,0:T(8,128)(2,1)S(1)}, ...), condition=%wide.region_7.0_spmd.clone, body=%wide.region_6.0_spmd.clone.sunk | while | flops 50790400 | bytes 1968312 | solution.py:91
  70.4 0.1 collective-permute-start
  70.5 0.2 fusion.51
  70.7 0.2 fusion.52
  70.9 1.7 collective-permute-start.1
  72.6 0.2 convolution_add_fusion.3
  72.8 2.1 collective-permute-done.1
  74.9 0.0 collective-permute-done
  74.9 0.1 collective-permute-start
  75.0 0.2 fusion.51
  75.2 0.2 fusion.52
  75.4 1.7 collective-permute-start.1
  77.1 0.2 convolution_add_fusion.3
  77.3 2.1 collective-permute-done.1
  79.4 0.0 collective-permute-done
  79.4 0.1 collective-permute-start
  79.5 0.2 fusion.51
  79.7 0.2 fusion.52
  79.9 1.7 collective-permute-start.1
  81.6 0.2 convolution_add_fusion.3
  81.8 2.1 collective-permute-done.1
  83.9 0.0 collective-permute-done
  83.9 0.1 collective-permute-start
  84.0 0.2 fusion.51
  84.2 0.2 fusion.52
  84.4 1.7 collective-permute-start.1
  86.1 0.2 convolution_add_fusion.3
  86.3 2.1 collective-permute-done.1
  88.4 0.0 collective-permute-done
  88.4 0.7 copy.41
  89.0 0.0 reduce-scatter.5.cloned.1.call-update
  89.1 0.0 reduce-scatter.7.cloned.1.call-start
  89.1 59.9 %reduce-scatter.5.cloned.1.call-done = bf16[8,4,128]{2,0,1:T(8,128)(2,1)} async-done(((bf16[8,32,128]{2,0,1:T(8,128)(2,1)}), bf16[8,4,128]{2,0,1:T(8,128)(2,1)}) %reduce-scatter.5.cloned.1.call-update) | async-done | bytes 8208 | tf_op jit(solution)/shard_map/reduce_scatter | solution.py:92
  149.0 1.0 convolution_bitcast_fusion.1
  150.0 0.3 fusion.13
  150.4 1.3 copy.45
  151.7 0.0 reduce-scatter.7.cloned.1.call-update
  151.8 1.4 fusion.12
  153.2 0.3 convolution_convert_fusion.1
  153.5 0.7 reshape.115
  154.2 133.5 %reduce-scatter.7.cloned.1.call-done = f32[64,128]{1,0:T(8,128)} async-done(((f32[2048,128]{1,0:T(8,128)}), f32[64,128]{1,0:T(8,128)}) %reduce-scatter.7.cloned.1.call-update) | async-done | bytes 32784
  (24 shorter events, 0.2 us)
Async XLA Ops:
  7.2 1.2 copy-start
  7.2 10.0 %copy-start.2 = (bf16[8,4,2048]{2,1,0:T(4,128)(2,1)S(1)}, bf16[8,4,2048]{2,1,0:T(4,128)(2,1)}, u32[]{:S(2)}) copy-start(bf16[8,4,2048]{2,1,0:T(4,128)(2,1)} %param.7) | copy-start | bytes 393220
  7.2 141.8 %reduce-scatter.5.cloned.1.call-start = ((), (), s32[]{:S(2)}) async-start(), calls=%async_computation.2 | async-start | bytes 73728 | tf_op jit(solution)/shard_map/reduce_scatter | solution.py:92
  8.4 8.8 %copy-start.1 = (bf16[2048,128]{1,0:T(8,128)(2,1)S(1)}, bf16[2048,128]{1,0:T(8,128)(2,1)}, u32[]{:S(2)}) copy-start(bf16[2048,128]{1,0:T(8,128)(2,1)} %param.9) | copy-start | bytes 1572868
  48.3 21.6 %copy-start.4 = (s32[8,8,2]{1,2,0:T(2,128)S(1)}, s32[8,8,2]{1,2,0:T(2,128)}, u32[]{:S(2)}) copy-start(s32[8,8,2]{1,2,0:T(2,128)} %param.10) | copy-start | bytes 1540
  48.4 21.7 %copy-start.5 = (s32[8,8]{1,0:T(8,128)S(1)}, s32[8,8]{1,0:T(8,128)}, u32[]{:S(2)}) copy-start(s32[8,8]{1,0:T(8,128)} %param.11) | copy-start | bytes 772
  70.4 4.5 %collective-permute-start = (bf16[1,256,128]{2,1,0:T(8,128)(2,1)S(1)}, bf16[1,256,128]{2,1,0:T(8,128)(2,1)S(1)}, u32[]{:S(2)}, u32[]{:S(2)}) collective-permute-start(bf16[1,256,128]{2,1,0:T(8,128)(2,1)S(1)} %copy.56), channel_id=1, source_target_pairs={{0,8},{8,16},{16,24},{24,0},{1,9},{9,17},{17,25},{25,1},{2,10},{10... | collective-permute-start | bytes 196616 | tf_op jit(solution)/shard_map/while/body/eval_jaxpr/ppermute | solution.py:12
  70.9 3.9 %collective-permute-start.1 = (bf16[1,256,128]{2,1,0:T(8,128)(2,1)S(1)}, bf16[1,256,128]{2,1,0:T(8,128)(2,1)S(1)}, u32[]{:S(2)}, u32[]{:S(2)}) collective-permute-start(bf16[1,256,128]{2,1,0:T(8,128)(2,1)S(1)} %fusion.52), channel_id=1, source_target_pairs={{0,8},{8,16},{16,24},{24,0},{1,9},{9,17},{17,25},{25,1},{2,10},{10... | collective-permute-start | bytes 196616 | tf_op jit(solution)/shard_map/while/body/eval_jaxpr/ppermute | solution.py:12
  74.9 4.5 %collective-permute-start = (bf16[1,256,128]{2,1,0:T(8,128)(2,1)S(1)}, bf16[1,256,128]{2,1,0:T(8,128)(2,1)S(1)}, u32[]{:S(2)}, u32[]{:S(2)}) collective-permute-start(bf16[1,256,128]{2,1,0:T(8,128)(2,1)S(1)} %copy.56), channel_id=1, source_target_pairs={{0,8},{8,16},{16,24},{24,0},{1,9},{9,17},{17,25},{25,1},{2,10},{10... | collective-permute-start | bytes 196616 | tf_op jit(solution)/shard_map/while/body/eval_jaxpr/ppermute | solution.py:12
  75.4 3.9 %collective-permute-start.1 = (bf16[1,256,128]{2,1,0:T(8,128)(2,1)S(1)}, bf16[1,256,128]{2,1,0:T(8,128)(2,1)S(1)}, u32[]{:S(2)}, u32[]{:S(2)}) collective-permute-start(bf16[1,256,128]{2,1,0:T(8,128)(2,1)S(1)} %fusion.52), channel_id=1, source_target_pairs={{0,8},{8,16},{16,24},{24,0},{1,9},{9,17},{17,25},{25,1},{2,10},{10... | collective-permute-start | bytes 196616 | tf_op jit(solution)/shard_map/while/body/eval_jaxpr/ppermute | solution.py:12
  79.4 4.5 %collective-permute-start = (bf16[1,256,128]{2,1,0:T(8,128)(2,1)S(1)}, bf16[1,256,128]{2,1,0:T(8,128)(2,1)S(1)}, u32[]{:S(2)}, u32[]{:S(2)}) collective-permute-start(bf16[1,256,128]{2,1,0:T(8,128)(2,1)S(1)} %copy.56), channel_id=1, source_target_pairs={{0,8},{8,16},{16,24},{24,0},{1,9},{9,17},{17,25},{25,1},{2,10},{10... | collective-permute-start | bytes 196616 | tf_op jit(solution)/shard_map/while/body/eval_jaxpr/ppermute | solution.py:12
  79.9 3.9 %collective-permute-start.1 = (bf16[1,256,128]{2,1,0:T(8,128)(2,1)S(1)}, bf16[1,256,128]{2,1,0:T(8,128)(2,1)S(1)}, u32[]{:S(2)}, u32[]{:S(2)}) collective-permute-start(bf16[1,256,128]{2,1,0:T(8,128)(2,1)S(1)} %fusion.52), channel_id=1, source_target_pairs={{0,8},{8,16},{16,24},{24,0},{1,9},{9,17},{17,25},{25,1},{2,10},{10... | collective-permute-start | bytes 196616 | tf_op jit(solution)/shard_map/while/body/eval_jaxpr/ppermute | solution.py:12
  83.9 4.5 %collective-permute-start = (bf16[1,256,128]{2,1,0:T(8,128)(2,1)S(1)}, bf16[1,256,128]{2,1,0:T(8,128)(2,1)S(1)}, u32[]{:S(2)}, u32[]{:S(2)}) collective-permute-start(bf16[1,256,128]{2,1,0:T(8,128)(2,1)S(1)} %copy.56), channel_id=1, source_target_pairs={{0,8},{8,16},{16,24},{24,0},{1,9},{9,17},{17,25},{25,1},{2,10},{10... | collective-permute-start | bytes 196616 | tf_op jit(solution)/shard_map/while/body/eval_jaxpr/ppermute | solution.py:12
  84.4 3.9 %collective-permute-start.1 = (bf16[1,256,128]{2,1,0:T(8,128)(2,1)S(1)}, bf16[1,256,128]{2,1,0:T(8,128)(2,1)S(1)}, u32[]{:S(2)}, u32[]{:S(2)}) collective-permute-start(bf16[1,256,128]{2,1,0:T(8,128)(2,1)S(1)} %fusion.52), channel_id=1, source_target_pairs={{0,8},{8,16},{16,24},{24,0},{1,9},{9,17},{17,25},{25,1},{2,10},{10... | collective-permute-start | bytes 196616 | tf_op jit(solution)/shard_map/while/body/eval_jaxpr/ppermute | solution.py:12
  89.1 198.6 %reduce-scatter.7.cloned.1.call-start = ((), (), s32[]{:S(2)}) async-start(), calls=%async_computation.3 | async-start | bytes 1081344
  151.7 1.4 copy-start.3
Sparse Core Ops, SparseCore 0:
  89.2 59.7 reduce-scatter.4
  151.9 135.8 reduce-scatter.6
where the time goes:
time: 295 us
  waiting for transfers between devices  202 us (68%)
  blocking collectives  58.6 us (20%)
  between operations  14.2 us (5%)
  matrix products  7.66 us (3%)
  starting transfers between devices  6.98 us (2%)
  local copies, waits for them, and re-layouts  4.37 us (1%)
    unnamed x3, waiting for transfers between devices  134 us
    reduce_scatter x1, waiting for transfers between devices, shards(): lax.psum_scatter(token_acc.reshape(query_count, query_tokens, embed_width...  59.9 us
    all_gather x1, blocking collectives, shards(): lax.all_gather(own_embed, 'pa', axis=1, tiled=True).reshape(-1, embed_width)  30.9 us
    all_gather x1, blocking collectives, shards(): score_table = lax.all_gather(query_score, 'pa', axis=1, tiled=True)  20.5 us
    ppermute x8, waiting for transfers between devices, from_behind(): return lax.ppermute(value, axis, pairs)  8.25 us
    all_gather x1, blocking collectives, shards(): lax.all_gather(page_embed, 'pb', axis=1, tiled=True)[0]  7.25 us
    ppermute x8, starting transfers between devices, from_behind(): return lax.ppermute(value, axis, pairs)  6.9 us
  transfers between devices with their start and end apart: 10, of which 6 were waited for; matrix products, arithmetic and copies ran while one was open for 2% of the time, Pallas kernels for 0%

commit v1 on v0

--- a/solution.py
+++ b/solution.py
@@ -4,6 +4,12 @@
 from jax.sharding import PartitionSpec as P
 
 sharpness = 0.25
+
+
+def gather_blocks(block, name, dim):
+    parts = lax.all_gather(block, name, axis=0, tiled=False)
+    result = jnp.concatenate(parts, axis=dim)
+    return result
 
 
 def from_behind(value, axis, steps):
@@ -26,7 +32,7 @@
         query_hidden.reshape(-1, hidden_width), projection, preferred_element_type=jnp.float32
     ).astype(jnp.bfloat16)
     own_embed = own_embed.reshape(query_count, token_local, embed_width)
-    tok_rows = lax.all_gather(own_embed, "pa", axis=1, tiled=True).reshape(-1, embed_width)
+    tok_rows = gather_blocks(own_embed, "pa", 1).reshape(-1, embed_width)
     row_count = tok_rows.shape[0]
     query_tokens = row_count // query_count
     page_embed = jnp.dot(

time: 295 us -> 295 us (level)
  no operation moved by 1% of the time
where the time goes in v1:
time: 295 us; the launch traced here: 294 us
  waiting for transfers between devices  202 us (68%)
  blocking collectives  58.6 us (20%)
  between operations  14.2 us (5%)
  matrix products  7.65 us (3%)
  starting transfers between devices  6.98 us (2%)
  local copies, waits for them, and re-layouts  4.39 us (1%)
    unnamed x3, waiting for transfers between devices  133 us
    reduce_scatter x1, waiting for transfers between devices, shards(): lax.psum_scatter(token_acc.reshape(query_count, query_tokens, embed_width...  59.9 us
    all_gather x1, blocking collectives, gather_blocks(): parts = lax.all_gather(block, name, axis=0, tiled=False)  30.9 us
    all_gather x1, blocking collectives, shards(): score_table = lax.all_gather(query_score, 'pa', axis=1, tiled=True)  20.5 us
    ppermute x8, waiting for transfers between devices, from_behind(): return lax.ppermute(value, axis, pairs)  8.26 us
    all_gather x1, blocking collectives, shards(): lax.all_gather(page_embed, 'pb', axis=1, tiled=True)[0]  7.25 us
    ppermute x8, starting transfers between devices, from_behind(): return lax.ppermute(value, axis, pairs)  6.9 us
  transfers between devices with their start and end apart: 10, of which 6 were waited for; matrix products, arithmetic and copies ran while one was open for 2% of the time, Pallas kernels for 0%

profile of v1, /device:TPU:0, one launch (start us, length us, event | category | flops | bytes accessed | tf_op | source)
XLA Modules:
  0.0 294.4 jit_solution(5023919623815478895)
XLA Ops:
  7.2 0.0 copy-start
  7.2 0.0 copy-start.2
  7.2 0.0 reduce-scatter.5.cloned.1.call-start
  7.2 1.2 copy-done
  8.4 1.5 convolution_convert_fusion.2
  9.9 7.3 %all-gather = bf16[1024,128]{1,0:T(8,128)(2,1)S(1)} all-gather(bf16[256,128]{1,0:T(8,128)(2,1)S(1)} %convolution_convert_fusion.2), channel_id=2, replica_groups=mesh['pb'=4,'pa'=8] {'pb'}, dimensions={0}, use_global_device_ids=true | all-gather | bytes 327680 | tf_op jit(solution)/shard_map/all_gather | solution.py:47
  17.2 0.0 copy-done.2
  17.2 0.2 convolution_convert_fusion.3
  17.5 30.9 %all_gather.9 = bf16[8,8,4,128]{3,1,2,0:T(8,128)(2,1)S(1)} all-gather(bf16[1,8,4,128]{3,1,2,0:T(8,128)(2,1)S(1)} %copy.38), channel_id=1, replica_groups=mesh['pb'=4,'pa'=8] {'pa'}, dimensions={0}, use_global_device_ids=true | all-gather | bytes 73728 | tf_op jit(solution)/shard_map/all_gather | solution.py:10
  48.4 0.0 copy-start.4
  48.4 0.0 copy-start.5
  48.4 0.4 fusion.24
  48.8 0.1 max_squeeze.20
  48.8 0.3 exponential_reduce_fusion
  49.2 0.1 reduce_sum.50
  49.3 0.1 add_reduce_fusion
  49.4 20.5 %all-gather.1 = f32[8,1,8]{2,1,0:T(1,128)S(1)} all-gather(f32[1,1,8]{2,1,0:T(1,128)S(1)} %bitcast.85), channel_id=1, replica_groups=mesh['pb'=4,'pa'=8] {'pa'}, dimensions={0}, use_global_device_ids=true | all-gather | bytes 288 | tf_op jit(solution)/shard_map/all_gather | solution.py:62
  69.8 0.1 copy.41
  69.9 0.2 select_reduce_fusion
  70.1 0.0 copy-done.5
  70.1 0.1 fusion.20
  70.2 0.1 broadcast_in_dim.24
  70.3 0.1 broadcast_in_dim.25
  70.4 18.0 %while.15 = (s32[]{:T(128)}, bf16[1,256,128]{2,1,0:T(8,128)(2,1)S(1)}, f32[1,256,128]{2,1,0:T(8,128)S(1)}, f32[256,128]{1,0:T(8,128)S(1)}, bf16[256,128]{1,0:T(8...) while((s32[]{:T(128)}, bf16[1,256,128]{2,1,0:T(8,128)(2,1)S(1)}, ...), condition=%wide.region_7.0_spmd.clone, body=%wide.region_6.0_spmd.clone.sunk | while | flops 50790400 | bytes 1968312 | solution.py:97
  70.4 0.1 collective-permute-start
  70.5 0.2 fusion.51
  70.7 0.2 fusion.52
  70.9 1.7 collective-permute-start.1
  72.6 0.2 convolution_add_fusion.3
  72.8 2.1 collective-permute-done.1
  74.9 0.0 collective-permute-done
  74.9 0.1 collective-permute-start
  75.0 0.2 fusion.51
  75.2 0.2 fusion.52
  75.4 1.7 collective-permute-start.1
  77.1 0.2 convolution_add_fusion.3
  77.3 2.1 collective-permute-done.1
  79.4 0.0 collective-permute-done
  79.4 0.1 collective-permute-start
  79.5 0.2 fusion.51
  79.7 0.2 fusion.52
  79.9 1.7 collective-permute-start.1
  81.6 0.2 convolution_add_fusion.3
  81.8 2.1 collective-permute-done.1
  83.9 0.0 collective-permute-done
  83.9 0.1 collective-permute-start
  84.0 0.2 fusion.51
  84.2 0.2 fusion.52
  84.4 1.7 collective-permute-start.1
  86.1 0.2 convolution_add_fusion.3
  86.3 2.1 collective-permute-done.1
  88.4 0.0 collective-permute-done
  88.4 0.7 copy.43
  89.1 0.0 reduce-scatter.5.cloned.1.call-update
  89.1 0.0 reduce-scatter.7.cloned.1.call-start
  89.1 59.9 %reduce-scatter.5.cloned.1.call-done = bf16[8,4,128]{2,0,1:T(8,128)(2,1)} async-done(((bf16[8,32,128]{2,0,1:T(8,128)(2,1)}), bf16[8,4,128]{2,0,1:T(8,128)(2,1)}) %reduce-scatter.5.cloned.1.call-update) | async-done | bytes 8208 | tf_op jit(solution)/shard_map/reduce_scatter | solution.py:98
  149.0 1.0 convolution_bitcast_fusion.1
  150.0 0.3 fusion.13
  150.4 1.3 copy.47
  151.7 0.0 reduce-scatter.7.cloned.1.call-update
  151.7 1.4 fusion.12
  153.2 0.3 convolution_convert_fusion.1
  153.4 0.7 reshape.111
  154.2 133.4 %reduce-scatter.7.cloned.1.call-done = f32[64,128]{1,0:T(8,128)} async-done(((f32[2048,128]{1,0:T(8,128)}), f32[64,128]{1,0:T(8,128)}) %reduce-scatter.7.cloned.1.call-update) | async-done | bytes 32784
  (24 shorter events, 0.2 us)
Async XLA Ops:
  7.2 1.2 copy-start
  7.2 10.0 %copy-start.2 = (bf16[8,4,2048]{2,1,0:T(4,128)(2,1)S(1)}, bf16[8,4,2048]{2,1,0:T(4,128)(2,1)}, u32[]{:S(2)}) copy-start(bf16[8,4,2048]{2,1,0:T(4,128)(2,1)} %param.7) | copy-start | bytes 393220
  7.2 141.8 %reduce-scatter.5.cloned.1.call-start = ((), (), s32[]{:S(2)}) async-start(), calls=%async_computation.2 | async-start | bytes 73728 | tf_op jit(solution)/shard_map/reduce_scatter | solution.py:98
  8.4 8.8 %copy-start.1 = (bf16[2048,128]{1,0:T(8,128)(2,1)S(1)}, bf16[2048,128]{1,0:T(8,128)(2,1)}, u32[]{:S(2)}) copy-start(bf16[2048,128]{1,0:T(8,128)(2,1)} %param.9) | copy-start | bytes 1572868
  48.4 21.6 %copy-start.4 = (s32[8,8,2]{1,2,0:T(2,128)S(1)}, s32[8,8,2]{1,2,0:T(2,128)}, u32[]{:S(2)}) copy-start(s32[8,8,2]{1,2,0:T(2,128)} %param.10) | copy-start | bytes 1540
  48.4 21.7 %copy-start.5 = (s32[8,8]{1,0:T(8,128)S(1)}, s32[8,8]{1,0:T(8,128)}, u32[]{:S(2)}) copy-start(s32[8,8]{1,0:T(8,128)} %param.11) | copy-start | bytes 772
  70.4 4.5 %collective-permute-start = (bf16[1,256,128]{2,1,0:T(8,128)(2,1)S(1)}, bf16[1,256,128]{2,1,0:T(8,128)(2,1)S(1)}, u32[]{:S(2)}, u32[]{:S(2)}) collective-permute-start(bf16[1,256,128]{2,1,0:T(8,128)(2,1)S(1)} %copy.58), channel_id=1, source_target_pairs={{0,8},{8,16},{16,24},{24,0},{1,9},{9,17},{17,25},{25,1},{2,10},{10... | collective-permute-start | bytes 196616 | tf_op jit(solution)/shard_map/while/body/eval_jaxpr/ppermute | solution.py:18
  70.9 3.9 %collective-permute-start.1 = (bf16[1,256,128]{2,1,0:T(8,128)(2,1)S(1)}, bf16[1,256,128]{2,1,0:T(8,128)(2,1)S(1)}, u32[]{:S(2)}, u32[]{:S(2)}) collective-permute-start(bf16[1,256,128]{2,1,0:T(8,128)(2,1)S(1)} %fusion.52), channel_id=1, source_target_pairs={{0,8},{8,16},{16,24},{24,0},{1,9},{9,17},{17,25},{25,1},{2,10},{10... | collective-permute-start | bytes 196616 | tf_op jit(solution)/shard_map/while/body/eval_jaxpr/ppermute | solution.py:18
  74.9 4.5 %collective-permute-start = (bf16[1,256,128]{2,1,0:T(8,128)(2,1)S(1)}, bf16[1,256,128]{2,1,0:T(8,128)(2,1)S(1)}, u32[]{:S(2)}, u32[]{:S(2)}) collective-permute-start(bf16[1,256,128]{2,1,0:T(8,128)(2,1)S(1)} %copy.58), channel_id=1, source_target_pairs={{0,8},{8,16},{16,24},{24,0},{1,9},{9,17},{17,25},{25,1},{2,10},{10... | collective-permute-start | bytes 196616 | tf_op jit(solution)/shard_map/while/body/eval_jaxpr/ppermute | solution.py:18
  75.4 3.9 %collective-permute-start.1 = (bf16[1,256,128]{2,1,0:T(8,128)(2,1)S(1)}, bf16[1,256,128]{2,1,0:T(8,128)(2,1)S(1)}, u32[]{:S(2)}, u32[]{:S(2)}) collective-permute-start(bf16[1,256,128]{2,1,0:T(8,128)(2,1)S(1)} %fusion.52), channel_id=1, source_target_pairs={{0,8},{8,16},{16,24},{24,0},{1,9},{9,17},{17,25},{25,1},{2,10},{10... | collective-permute-start | bytes 196616 | tf_op jit(solution)/shard_map/while/body/eval_jaxpr/ppermute | solution.py:18
  79.4 4.5 %collective-permute-start = (bf16[1,256,128]{2,1,0:T(8,128)(2,1)S(1)}, bf16[1,256,128]{2,1,0:T(8,128)(2,1)S(1)}, u32[]{:S(2)}, u32[]{:S(2)}) collective-permute-start(bf16[1,256,128]{2,1,0:T(8,128)(2,1)S(1)} %copy.58), channel_id=1, source_target_pairs={{0,8},{8,16},{16,24},{24,0},{1,9},{9,17},{17,25},{25,1},{2,10},{10... | collective-permute-start | bytes 196616 | tf_op jit(solution)/shard_map/while/body/eval_jaxpr/ppermute | solution.py:18
  79.9 3.9 %collective-permute-start.1 = (bf16[1,256,128]{2,1,0:T(8,128)(2,1)S(1)}, bf16[1,256,128]{2,1,0:T(8,128)(2,1)S(1)}, u32[]{:S(2)}, u32[]{:S(2)}) collective-permute-start(bf16[1,256,128]{2,1,0:T(8,128)(2,1)S(1)} %fusion.52), channel_id=1, source_target_pairs={{0,8},{8,16},{16,24},{24,0},{1,9},{9,17},{17,25},{25,1},{2,10},{10... | collective-permute-start | bytes 196616 | tf_op jit(solution)/shard_map/while/body/eval_jaxpr/ppermute | solution.py:18
  83.9 4.5 %collective-permute-start = (bf16[1,256,128]{2,1,0:T(8,128)(2,1)S(1)}, bf16[1,256,128]{2,1,0:T(8,128)(2,1)S(1)}, u32[]{:S(2)}, u32[]{:S(2)}) collective-permute-start(bf16[1,256,128]{2,1,0:T(8,128)(2,1)S(1)} %copy.58), channel_id=1, source_target_pairs={{0,8},{8,16},{16,24},{24,0},{1,9},{9,17},{17,25},{25,1},{2,10},{10... | collective-permute-start | bytes 196616 | tf_op jit(solution)/shard_map/while/body/eval_jaxpr/ppermute | solution.py:18
  84.4 3.9 %collective-permute-start.1 = (bf16[1,256,128]{2,1,0:T(8,128)(2,1)S(1)}, bf16[1,256,128]{2,1,0:T(8,128)(2,1)S(1)}, u32[]{:S(2)}, u32[]{:S(2)}) collective-permute-start(bf16[1,256,128]{2,1,0:T(8,128)(2,1)S(1)} %fusion.52), channel_id=1, source_target_pairs={{0,8},{8,16},{16,24},{24,0},{1,9},{9,17},{17,25},{25,1},{2,10},{10... | collective-permute-start | bytes 196616 | tf_op jit(solution)/shard_map/while/body/eval_jaxpr/ppermute | solution.py:18
  89.1 198.5 %reduce-scatter.7.cloned.1.call-start = ((), (), s32[]{:S(2)}) async-start(), calls=%async_computation.3 | async-start | bytes 1081344
  151.7 1.4 copy-start.3
Sparse Core Ops, SparseCore 0:
  89.2 59.7 reduce-scatter.4
  151.9 135.6 reduce-scatter.6
